TPU v7x, 32 devices: a whole 2x2x4 slice. The times are simulated.
32 devices in a mesh: slides: 2 (over y), row: 16 (over z, x, core).
Axes of the slice: x: 2, y: 2, z: 4, core: 2. Of those that a mesh axis runs over, the one named last changes fastest.
Arguments:
- slide_pixels: bfloat16 [2048, 16384], P(('slides', 'row')), parts along dimension 0, may hold values from -6 to 6
- tissue_mask: int32 [64, 8], P(('slides', 'row')), parts along dimension 0, may hold values from 0 to 1, as said below
- conv_weight: bfloat16 [3, 3, 64, 64], replicated, may hold values from -0.25 to 0.25
- conv_bias: bfloat16 [64], replicated, may hold values from -3 to 3
Outputs:
- packed_tiles: bfloat16 [256, 32, 2048], P(('slides', 'row')), parts along dimension 0
There are 2 independent parts, one for each index of `slides`. A program takes and returns all parts, laid end to end along the dimension named above; an argument that names none is the same for every part. Nothing has to cross between parts.
Inputs may be any that keep to these rules, and one draw needn't show every extreme that they name: `tissue_mask`: exactly 128 tiles hold tissue. For every s from 1 to 15, the first s * 2 tile rows hold s * 8 + e tissue tiles with e between 0 and 2; e = 2 occurs in every draw. For every such s, some column holds tissue in both tile row s * 2 - 1 and tile row s * 2.
All inputs are finite; a program needn't handle non-finite values.
Results may differ from a plain program's by a relative error of at most 0.001.
Values may be sent and summed in bfloat16 or wider, within the bound.
A program may use at most 64 MiB of HBM per device.

v0:
```python
import functools

import jax
import jax.numpy as jnp
from jax import lax
from jax.experimental import pallas as pl
from jax.experimental.pallas import tpu as pltpu
from jax.sharding import PartitionSpec as P

SLOTS = 8
SHIFT_MOST = 2
LANES = 128
PACK = 16
MESH = pl.DeviceIdType.MESH


def kernel(
    n, side, channels,
    x_ref, mask_s, mask_v, w_ref, b_ref, out_any,
    image, conv, low, rows3, wide, masks, stage_up, stage_dn, halo_top, halo_bot, onward, arrived,
    x_sem, mask_send, mask_recv, halo_send, halo_recv, tile_send, tile_recv,
    out_ref, out_sem,
):
    band_rows, cols = mask_s.shape
    height = band_rows * side
    width = side * channels
    tiles = band_rows * cols
    quad = 2 * LANES
    groups = width // quad
    per = quad // channels
    half = LANES // channels
    me = lax.axis_index("row")

    barrier = pltpu.get_barrier_semaphore()

    def greet(j, carry):
        pl.semaphore_signal(
            barrier, inc=1, device_id={"row": lax.rem(me + j, n)}, device_id_type=MESH
        )
        return carry

    lax.fori_loop(1, n, greet, 0)

    def fetch(c):
        return pltpu.make_async_copy(
            x_ref.at[:, pl.ds(c * width, width)],
            image.at[pl.ds(PACK, height), pl.ds(LANES + c * width, width)],
            x_sem.at[c],
        )

    for c in range(cols):
        fetch(c).start()

    none = jnp.zeros((channels, channels), jnp.bfloat16)
    for dy in range(3):
        taps = [w_ref[dy, 0], w_ref[dy, 1], w_ref[dy, 2]]
        for p in range(2 * per):
            for q in range(per // half):
                u = p - half - half * q
                parts = [taps[u + 1 - o] if 0 <= u + 1 - o <= 2 else none for o in range(half)]
                wide[dy, p * channels:(p + 1) * channels, q * LANES:(q + 1) * LANES] = (
                    jnp.concatenate(parts, axis=1)
                )
    edge = jnp.zeros((height + 2 * PACK, LANES), jnp.bfloat16)
    image[:, 0:LANES] = edge
    image[:, LANES + cols * width:2 * LANES + cols * width] = edge
    masks[me] = mask_v[...]
    blank_rows = jnp.zeros((PACK, cols * width), jnp.bfloat16)
    image[0:PACK, LANES:LANES + cols * width] = blank_rows
    image[PACK + height:2 * PACK + height, LANES:LANES + cols * width] = blank_rows

    firsts, lasts = [], []
    for c in range(cols):
        fetch(c).wait()
        for r in range(band_rows):
            keep = jnp.full((side, LANES), mask_s[r, c], jnp.int32).astype(jnp.float32)
            keep = keep.astype(jnp.bfloat16)
            for k in range(width // LANES):
                at = (pl.ds(PACK + r * side, side), pl.ds(LANES + c * width + k * LANES, LANES))
                image[at] = image[at] * keep
        span = pl.ds(LANES + c * width, width)
        first = image[PACK:2 * PACK, span].astype(jnp.float32)
        last = image[height:height + PACK, span].astype(jnp.float32)
        firsts.append(first[0:1])
        lasts.append(last[PACK - 1:PACK])
    stage_up[...] = jnp.concatenate(firsts, axis=0).astype(jnp.bfloat16)
    stage_dn[...] = jnp.concatenate(lasts, axis=0).astype(jnp.bfloat16)

    pl.semaphore_wait(barrier, n - 1)

    down = pltpu.make_async_remote_copy(
        stage_dn, halo_top, halo_send.at[0], halo_recv.at[0],
        device_id={"row": lax.rem(me + 1, n)}, device_id_type=MESH)
    up = pltpu.make_async_remote_copy(
        stage_up, halo_bot, halo_send.at[1], halo_recv.at[1],
        device_id={"row": lax.rem(me + n - 1, n)}, device_id_type=MESH)
    is_first = me == 0
    is_last = me == n - 1

    @pl.when(jnp.logical_not(is_last))
    def _():
        down.start()

    @pl.when(jnp.logical_not(is_first))
    def _():
        up.start()

    def mask_copy(target, slot):
        return pltpu.make_async_remote_copy(
            mask_v, masks.at[slot], mask_send.at[target], mask_recv.at[slot],
            device_id={"row": target}, device_id_type=MESH)

    def tell(j, carry):
        mask_copy(lax.rem(me + j, n), me).start()
        return carry

    lax.fori_loop(1, n, tell, 0)

    bias = b_ref[...].astype(jnp.float32)
    bias = jnp.concatenate([bias] * per, axis=1)
    duo = 2
    duos = cols // duo
    bands = duo * groups

    def convolve(r, pair, carry):
        left = pl.multiple_of(pair * (duo * width), duo * width)
        for k in range(bands + 1):
            block = image[r * side:(r + 1) * side + 2 * PACK, pl.ds(left + k * quad, quad)]
            span = pl.ds(k * quad, quad)
            block32 = block.astype(jnp.float32)
            rows3[0, :, span] = block32[PACK - 1:PACK - 1 + side].astype(jnp.bfloat16)
            rows3[1, :, span] = block[PACK:PACK + side]
            rows3[2, :, span] = block32[PACK + 1:PACK + 1 + side].astype(jnp.bfloat16)
        left_side = jnp.concatenate([jnp.concatenate(
            [rows3[dy, :, g * quad:(g + 2) * quad] for g in range(bands)], axis=0)
            for dy in range(3)], axis=1)
        total = jnp.dot(left_side, wide[...].reshape(6 * quad, quad),
            preferred_element_type=jnp.float32) + bias
        done = total.astype(jnp.bfloat16)
        for g in range(bands):
            at = g % groups * quad
            tile_at = r * cols + pair * duo + g // groups
            conv[tile_at, :, at:at + quad] = done[g * side:(g + 1) * side]
            if r == band_rows - 1:
                low[pair * duo + g // groups, :, at:at + quad] = (
                    total[(g + 1) * side - 8:(g + 1) * side])
        return carry

    lax.fori_loop(0, duos, functools.partial(convolve, band_rows - 1), 0)

    @pl.when(jnp.logical_not(is_first))
    def _():
        down.wait_recv()
        lines = halo_top[...].astype(jnp.float32)
        for c in range(cols):
            image[0:PACK, LANES + c * width:LANES + (c + 1) * width] = (
                jnp.broadcast_to(lines[c:c + 1], (PACK, width)).astype(jnp.bfloat16))

    for r in range(band_rows - 2, 0, -1):
        lax.fori_loop(0, duos, functools.partial(convolve, r), 0)
    lax.fori_loop(duos - 1, duos, functools.partial(convolve, 0), 0)

    @pl.when(jnp.logical_not(is_last))
    def _():
        up.wait_recv()
        lines = halo_bot[...].astype(jnp.float32)
        blank = jnp.zeros((1, LANES), jnp.float32)
        before = jnp.concatenate([blank, lines[0:cols - 1, width - LANES:width]], axis=0)
        after = jnp.concatenate([lines[1:cols, 0:LANES], blank], axis=0)
        lines = jnp.concatenate([before, lines, after], axis=1)
        stack = jnp.concatenate(
            [lines[:, g * quad:(g + 2) * quad] for g in range(groups)], axis=0)
        more = jnp.dot(
            stack.astype(jnp.bfloat16), wide[2], preferred_element_type=jnp.float32)
        lowest = lax.broadcasted_iota(jnp.int32, (PACK, quad), 0) == PACK - 1
        for c in range(cols):
            for g in range(groups):
                at = g * quad
                row = low[c, 7:8, at:at + quad] + more[g * cols + c:g * cols + c + 1]
                where = ((band_rows - 1) * cols + c, pl.ds(side - PACK, PACK), pl.ds(at, quad))
                old = conv[where].astype(jnp.float32)
                new = jnp.where(lowest, jnp.broadcast_to(row, (PACK, quad)), old)
                conv[where] = new.astype(jnp.bfloat16)

    seen = []
    for r in range(band_rows):
        for c in range(cols):
            seen.append(mask_s[r, c] + (seen[-1] if seen else 0))

    def place(rank):
        total = jnp.int32(0)
        for count in seen:
            total = total + jnp.where(count <= rank, 1, 0)
        return jnp.minimum(total, tiles - 1)

    for k in range(SHIFT_MOST):
        onward[k] = conv[place(seen[-1] - SHIFT_MOST + k)]
    tile = pltpu.make_async_remote_copy(
        onward, arrived, tile_send, tile_recv,
        device_id={"row": lax.rem(me + 1, n)}, device_id_type=MESH)

    @pl.when(jnp.logical_not(is_last))
    def _():
        tile.start()

    lax.fori_loop(0, duos - 1, functools.partial(convolve, 0), 0)

    def told(j, carry):
        mask_copy(lax.rem(me + j, n), lax.rem(me + j, n)).wait_recv()
        return carry

    lax.fori_loop(1, n, told, 0)
    device = lax.broadcasted_iota(jnp.int32, masks.shape, 0)
    excess = jnp.sum(jnp.where(device < me, masks[...], 0)) - SLOTS * me

    def give(k):
        return pltpu.make_async_copy(out_ref.at[k], out_any.at[k], out_sem.at[k])

    for k in range(SHIFT_MOST, SLOTS):
        out_ref[k] = conv[place(k - excess)]
        give(k).start()
    for k in range(SHIFT_MOST):
        out_ref[k] = conv[place(k - excess)]

    @pl.when(jnp.logical_not(is_first))
    def _():
        tile.wait_recv()
        late_at = [
            jnp.minimum(k + SHIFT_MOST - jnp.clip(excess, 0, SHIFT_MOST), SHIFT_MOST - 1)
            for k in range(SHIFT_MOST)
        ]
        for k in range(SHIFT_MOST):
            own = out_ref[k].astype(jnp.float32)
            theirs = arrived[late_at[k]].astype(jnp.float32)
            late = jnp.full(own.shape, excess, jnp.int32) > k
            out_ref[k] = jnp.where(late, theirs, own).astype(jnp.bfloat16)
        up.wait_send()

    for k in range(SHIFT_MOST):
        give(k).start()

    @pl.when(jnp.logical_not(is_last))
    def _():
        down.wait_send()
        tile.wait_send()

    def sent(j, carry):
        mask_copy(lax.rem(me + j, n), me).wait_send()
        return carry

    lax.fori_loop(1, n, sent, 0)
    for k in range(SLOTS):
        give(k).wait()


def hand_on(in_ref, out_ref, held, in_sem, out_sem):
    def take(k):
        return pltpu.make_async_copy(in_ref.at[k], held.at[k], in_sem.at[k])

    def give(k):
        return pltpu.make_async_copy(held.at[k], out_ref.at[k], out_sem.at[k])

    for k in range(SLOTS):
        take(k).start()
    for k in range(SLOTS):
        take(k).wait()
        give(k).start()
    for k in range(SLOTS):
        give(k).wait()


def on_device(slide_pixels, tissue_mask, conv_weight, conv_bias):
    n = lax.axis_size("row")
    band_rows, cols = tissue_mask.shape
    channels = conv_weight.shape[2]
    height = slide_pixels.shape[0]
    side = height // band_rows
    width = side * channels
    quad = 2 * LANES
    vmem = pl.BlockSpec(memory_space=pltpu.VMEM)
    bf16 = jnp.bfloat16
    tiles = pl.pallas_call(
        functools.partial(kernel, n, side, channels),
        out_shape=jax.ShapeDtypeStruct((SLOTS, side, width), bf16),
        in_specs=[
            pl.BlockSpec(memory_space=pl.ANY),
            pl.BlockSpec(memory_space=pltpu.SMEM),
            vmem, vmem, vmem,
        ],
        out_specs=pl.BlockSpec(memory_space=pl.ANY),
        scratch_shapes=[
            pltpu.VMEM((height + 2 * PACK, cols * width + 2 * LANES), bf16),
            pltpu.VMEM((band_rows * cols, side, width), bf16),
            pltpu.VMEM((cols, 8, width), jnp.float32),
            pltpu.VMEM((3, side, 2 * width + quad), bf16),
            pltpu.VMEM((3, 2 * quad, quad), bf16),
            pltpu.VMEM((n, band_rows, cols), jnp.int32),
            pltpu.VMEM((cols, width), bf16),
            pltpu.VMEM((cols, width), bf16),
            pltpu.VMEM((cols, width), bf16),
            pltpu.VMEM((cols, width), bf16),
            pltpu.VMEM((SHIFT_MOST, side, width), bf16),
            pltpu.VMEM((SHIFT_MOST, side, width), bf16),
            pltpu.SemaphoreType.DMA((cols,)),
            pltpu.SemaphoreType.DMA((n,)),
            pltpu.SemaphoreType.DMA((n,)),
            pltpu.SemaphoreType.DMA((2,)),
            pltpu.SemaphoreType.DMA((2,)),
            pltpu.SemaphoreType.DMA,
            pltpu.SemaphoreType.DMA,
            pltpu.VMEM((SLOTS, side, width), bf16),
            pltpu.SemaphoreType.DMA((SLOTS,)),
        ],
        compiler_params=pltpu.CompilerParams(collective_id=0, has_side_effects=True),
    )(slide_pixels, tissue_mask, tissue_mask, conv_weight, conv_bias.reshape(1, channels))
    return pl.pallas_call(
        hand_on,
        out_shape=jax.ShapeDtypeStruct(tiles.shape, bf16),
        in_specs=[pl.BlockSpec(memory_space=pl.ANY)],
        out_specs=pl.BlockSpec(memory_space=pl.ANY),
        scratch_shapes=[
            pltpu.VMEM(tiles.shape, bf16),
            pltpu.SemaphoreType.DMA((SLOTS,)),
            pltpu.SemaphoreType.DMA((SLOTS,)),
        ],
    )(tiles)


def solution(mesh):
    return jax.shard_map(
        on_device,
        mesh=mesh,
        in_specs=(P(("slides", "row"), None), P(("slides", "row"), None), P(), P()),
        out_specs=P(("slides", "row"), None, None),
        check_vma=False,
    )
```

profile of v0, /device:TPU:8, one launch (start us, length us, event | category | flops | bytes accessed | tf_op | source)
XLA Modules:
  0.0 16.8 jit_solution(1938597655867210769)
XLA Ops:
  0.0 14.7 %shard_map.46.in_ref = bf16[8,32,2048]{2,1,0:T(8,128)(2,1)} custom-call(bf16[64,16384]{1,0:T(8,128)(2,1)} %x_ref.1, s32[2,8]{1,0:T(2,128)} %mask_v.1, s32[2,8]{1,0:T(2,128)} %mask_v.1, bf16[3,3,64,64]{3,2,1,0:T(8,128)(2,1)} %w_ref.1, bf16[1,64]{1,0:T(2,128)(2,1)} %bitcast.1), custom_call_target="tpu_custom_call" | custom-call | tf_op jit(solution)/shard_map/pallas_call | solution.py:282
  14.7 2.1 %shard_map.47 = bf16[8,32,2048]{2,1,0:T(8,128)(2,1)} custom-call(bf16[8,32,2048]{2,1,0:T(8,128)(2,1)} %shard_map.46.in_ref), custom_call_target="tpu_custom_call" | custom-call | tf_op jit(solution)/shard_map/pallas_call | solution.py:316
where the time goes:
time: 16.9 us; the launch traced here: 16.8 us
  Pallas kernels  16.7 us (99%)
    pallas_call x1, Pallas kernels, on_device(): pl.pallas_call(functools.partial(kernel, n, side, channels), out_shape=ja...  14.7 us
    pallas_call x1, Pallas kernels, on_device(): pl.pallas_call(hand_on, out_shape=jax.ShapeDtypeStruct(tiles.shape, bf16)...  2.09 us

commit v1 on v0

v1 whole, which is shorter than its diff:
```python
import functools
import math

import jax
import jax.numpy as jnp
from jax import lax
from jax.experimental import pallas as pl
from jax.experimental.pallas import tpu as pltpu
from jax.sharding import PartitionSpec as P

SLOTS = 8
SHIFT_MOST = 2
LANES = 128
PACK = 16
GROUP = 4
MESH = pl.DeviceIdType.MESH


def kernel(
    n, side, channels,
    x_any, mask_any, w_any, b_any, out_ref,
    image, own, rows3, wide, w_ref, b_ref, mask_s,
    row_first, row_second, row_late, row_last, halo_top, halo_bot,
    onward, arrived, edge, rim_out, rim_in, tally, chain_in, group_out, group_in,
    x_sem, in_sem, halo_send, halo_recv, tile_send, tile_recv, rim_send, rim_recv,
    chain_send, chain_recv, group_send, group_recv,
):
    band_rows, cols = mask_s.shape
    height = band_rows * side
    width = side * channels
    tiles = band_rows * cols
    quad = 2 * LANES
    groups = width // quad
    per = quad // channels
    half = LANES // channels
    team = math.gcd(n, GROUP)
    me = lax.axis_index("row")
    seat = lax.rem(me, team)
    base = me - seat
    deep = lax.div(base, team)
    is_first = me == 0
    is_last = me == n - 1
    has_back = me >= team
    has_ahead = me + team < n

    barrier = pltpu.get_barrier_semaphore()

    def greet(target):
        pl.semaphore_signal(barrier, inc=1, device_id={"row": target}, device_id_type=MESH)

    for j in range(1, team):
        greet(base + lax.rem(seat + j, team))

    @pl.when(jnp.logical_and(seat == 0, jnp.logical_not(is_first)))
    def _():
        greet(me - 1)

    @pl.when(jnp.logical_and(seat == team - 1, jnp.logical_not(is_last)))
    def _():
        greet(me + 1)

    @pl.when(has_back)
    def _():
        greet(me - team)

    def fetch(r, c):
        return pltpu.make_async_copy(
            x_any.at[pl.ds(r * side, side), pl.ds(c * width, width)],
            image.at[r + 1, c + 1],
            x_sem.at[r * cols + c],
        )

    get_mask = pltpu.make_async_copy(mask_any, mask_s, in_sem.at[0])
    get_w = pltpu.make_async_copy(w_any, w_ref, in_sem.at[1])
    get_b = pltpu.make_async_copy(b_any, b_ref, in_sem.at[2])
    get_mask.start()
    get_w.start()
    get_b.start()
    for c in range(cols):
        for r in range(band_rows):
            fetch(r, c).start()

    for r in range(1, band_rows + 1):
        image[r, 0, :, width - LANES:width] = jnp.zeros((side, LANES), jnp.bfloat16)
        image[r, cols + 1, :, 0:LANES] = jnp.zeros((side, LANES), jnp.bfloat16)
    for c in range(cols + 2):
        image[0, c, side - PACK:side, :] = jnp.zeros((PACK, width), jnp.bfloat16)
        image[band_rows + 1, c, 0:PACK, :] = jnp.zeros((PACK, width), jnp.bfloat16)

    @pl.when(is_first)
    def _():
        halo_top[...] = jnp.zeros_like(halo_top)

    @pl.when(is_last)
    def _():
        halo_bot[...] = jnp.zeros_like(halo_bot)

    get_mask.wait()
    seen = []
    for r in range(band_rows):
        for c in range(cols):
            seen.append(mask_s[r, c] + (seen[-1] if seen else 0))
    count = seen[-1]

    def place(rank):
        spot = jnp.int32(0)
        row = jnp.int32(0)
        for t in range(tiles - 1):
            past = jnp.where(seen[t] <= rank, 1, 0)
            spot = spot + past
            if t % cols == cols - 1:
                row = row + past
        return row, spot - row * cols

    get_w.wait()
    none = jnp.zeros((channels, channels), jnp.bfloat16)
    for dy in range(3):
        taps = [w_ref[dy, 0], w_ref[dy, 1], w_ref[dy, 2]]
        for p in range(2 * per):
            for q in range(per // half):
                u = p - half - half * q
                parts = [taps[u + 1 - o] if 0 <= u + 1 - o <= 2 else none for o in range(half)]
                wide[dy, p * channels:(p + 1) * channels, q * LANES:(q + 1) * LANES] = (
                    jnp.concatenate(parts, axis=1)
                )
    get_b.wait()
    bias = b_ref[...].astype(jnp.float32)
    bias = jnp.concatenate([bias] * per, axis=1)

    lines = [[], [], [], []]
    for c in range(cols):
        for r in range(band_rows):
            fetch(r, c).wait()
            keep = jnp.full((side, LANES), mask_s[r, c], jnp.int32).astype(jnp.float32)
            keep = keep.astype(jnp.bfloat16)
            for k in range(width // LANES):
                at = (r + 1, c + 1, slice(None), pl.ds(k * LANES, LANES))
                image[at] = image[at] * keep
        first = image[1, c + 1, 0:PACK].astype(jnp.float32)
        last = image[band_rows, c + 1, side - PACK:side].astype(jnp.float32)
        lines[0].append(first[0:1])
        lines[1].append(first[1:2])
        lines[2].append(last[PACK - 2:PACK - 1])
        lines[3].append(last[PACK - 1:PACK])
    for ref, found in zip((row_first, row_second, row_late, row_last), lines):
        ref[...] = jnp.concatenate(found, axis=0).astype(jnp.bfloat16)

    tally[...] = jnp.full(tally.shape, count, jnp.int32)

    outside = jnp.logical_or(
        jnp.logical_and(seat == 0, jnp.logical_not(is_first)),
        jnp.logical_and(seat == team - 1, jnp.logical_not(is_last)))
    pl.semaphore_wait(
        barrier, team - 1 + jnp.where(outside, 1, 0) + jnp.where(has_ahead, 1, 0))

    ahead = {"row": lax.rem(me + 1, n)}
    behind = {"row": lax.rem(me + n - 1, n)}
    down = pltpu.make_async_remote_copy(
        row_last, halo_top, halo_send.at[0], halo_recv.at[0],
        device_id=ahead, device_id_type=MESH)
    up = pltpu.make_async_remote_copy(
        row_first, halo_bot, halo_send.at[1], halo_recv.at[1],
        device_id=behind, device_id_type=MESH)
    relay = pltpu.make_async_remote_copy(
        tally, chain_in, chain_send, chain_recv,
        device_id={"row": lax.rem(me + team, n)}, device_id_type=MESH)

    def tile(k):
        return pltpu.make_async_remote_copy(
            onward.at[k], arrived.at[k], tile_send.at[k], tile_recv.at[k],
            device_id=ahead, device_id_type=MESH)

    rims = pltpu.make_async_remote_copy(
        rim_out, rim_in, rim_send, rim_recv, device_id=ahead, device_id_type=MESH)

    def share(target, slot):
        return pltpu.make_async_remote_copy(
            group_out, group_in.at[slot], group_send.at[target], group_recv.at[slot],
            device_id={"row": base + target}, device_id_type=MESH)

    @pl.when(jnp.logical_not(is_first))
    def _():
        up.start()

    @pl.when(jnp.logical_not(is_last))
    def _():
        down.start()

    upper = lax.broadcasted_iota(jnp.int32, tally.shape, 0) < tally.shape[0] // 2

    def spread(before):
        group_out[...] = jnp.where(upper, before, tally[...])
        for j in range(1, team):
            share(lax.rem(seat + j, team), seat).start()

    @pl.when(jnp.logical_not(has_back))
    def _():
        @pl.when(has_ahead)
        def _():
            relay.start()
        spread(jnp.zeros(tally.shape, jnp.int32))

    def pass_on():
        relay.wait_recv()
        spread(chain_in[...])
        tally[...] = chain_in[...] + tally[...]

        @pl.when(has_ahead)
        def _():
            relay.start()

    def convolve(spots, put):
        for i, (r, c) in enumerate(spots):
            for k in range(width // LANES + 2):
                if k == 0:
                    at, lane = c, width - LANES
                elif k <= width // LANES:
                    at, lane = c + 1, (k - 1) * LANES
                else:
                    at, lane = c + 2, 0
                lane = slice(lane, lane + LANES)
                block = image[r + 1, at, :, lane]
                above = image[r, at, side - PACK:side, lane].astype(jnp.float32)
                below = image[r + 2, at, 0:PACK, lane].astype(jnp.float32)
                block32 = block.astype(jnp.float32)
                span = pl.ds(i * (groups + 1) * quad + k * LANES, LANES)
                rows3[0, :, span] = jnp.concatenate(
                    [above[PACK - 1:PACK], block32[0:side - 1]], axis=0).astype(jnp.bfloat16)
                rows3[1, :, span] = block
                rows3[2, :, span] = jnp.concatenate(
                    [block32[1:side], below[0:1]], axis=0).astype(jnp.bfloat16)
        starts = [(i * (groups + 1) + g) * quad for i in range(len(spots)) for g in range(groups)]
        left_side = jnp.concatenate([jnp.concatenate(
            [rows3[dy, :, s:s + 2 * quad] for s in starts], axis=0)
            for dy in range(3)], axis=1)
        total = jnp.dot(left_side, wide[...].reshape(6 * quad, quad),
            preferred_element_type=jnp.float32) + bias
        done = total.astype(jnp.bfloat16)
        for i in range(len(spots)):
            for g in range(groups):
                at = (i * groups + g) * side
                put(i, g, done[at:at + side])

    leaving = [place(count - SHIFT_MOST + k) for k in range(SHIFT_MOST)]
    for k in range(SHIFT_MOST):
        def put_onward(i, g, value, k=k):
            onward[k, :, g * quad:(g + 1) * quad] = value

        convolve([leaving[k]], put_onward)

        @pl.when(jnp.logical_not(is_last))
        def _(k=k):
            tile(k).start()

    duo = 2
    duos = SLOTS // duo
    turn = (deep - 1) * 2

    def several(j, carry):
        @pl.when(jnp.logical_and(has_back, turn == j))
        def _():
            pass_on()

        def put_own(i, g, value):
            own[j * duo + i, :, g * quad:(g + 1) * quad] = value

        convolve([place(j * duo + i) for i in range(duo)], put_own)
        return carry

    lax.fori_loop(0, duos, several, 0)

    @pl.when(jnp.logical_and(has_back, turn >= duos))
    def _():
        pass_on()

    @pl.when(jnp.logical_not(is_first))
    def _():
        down.wait_recv()

    @pl.when(jnp.logical_not(is_last))
    def _():
        up.wait_recv()

    sides = []
    for trio in ((halo_top, row_first, row_second), (row_late, row_last, halo_bot)):
        parts = []
        for ref in trio:
            line = ref[...].astype(jnp.float32)
            blank = jnp.zeros((1, LANES), jnp.float32)
            before = jnp.concatenate([blank, line[0:cols - 1, width - LANES:width]], axis=0)
            after = jnp.concatenate([line[1:cols, 0:LANES], blank], axis=0)
            line = jnp.concatenate([before, line, after], axis=1)
            parts.append(jnp.concatenate(
                [line[:, g * quad:(g + 2) * quad] for g in range(groups)], axis=0))
        sides.append(jnp.concatenate(parts, axis=1))
    rim = jnp.dot(
        jnp.concatenate(sides, axis=0).astype(jnp.bfloat16), wide[...].reshape(6 * quad, quad),
        preferred_element_type=jnp.float32) + bias
    for s in range(2):
        for g in range(groups):
            at = (s * groups + g) * cols
            for c in range(cols):
                edge[s, c, :, g * quad:(g + 1) * quad] = rim[at + c:at + c + 1]

    ends = []
    for k in range(SHIFT_MOST):
        r, c = leaving[k]
        at_top = jnp.full((1, width), r, jnp.int32) == 0
        at_end = jnp.full((1, width), r, jnp.int32) == band_rows - 1
        ends.append(jnp.where(
            at_top, edge[0, c], onward[k, 0:PACK].astype(jnp.float32)[0:1]))
        ends.append(jnp.where(
            at_end, edge[1, c],
            onward[k, side - PACK:side].astype(jnp.float32)[PACK - 1:PACK]))
    rim_out[...] = jnp.concatenate(ends, axis=0).astype(jnp.bfloat16)

    @pl.when(jnp.logical_not(is_last))
    def _():
        rims.start()

    line_at = lax.broadcasted_iota(jnp.int32, (PACK, quad), 0)

    def finish(j, carry):
        r, c = place(j)
        rows = jnp.full((PACK, quad), r, jnp.int32)
        at_top = jnp.logical_and(rows == 0, line_at == 0)
        at_end = jnp.logical_and(rows == band_rows - 1, line_at == PACK - 1)
        for g in range(groups):
            span = pl.ds(g * quad, quad)
            for s, where, at in ((0, at_top, 0), (1, at_end, side - PACK)):
                old = own[j, at:at + PACK, span].astype(jnp.float32)
                new = jnp.broadcast_to(edge[s, c, :, span], (PACK, quad))
                own[j, at:at + PACK, span] = jnp.where(where, new, old).astype(jnp.bfloat16)
        return carry

    lax.fori_loop(0, SLOTS, finish, 0)

    sum_of = group_out[...] * jnp.where(upper, 1, 0)
    for j in range(1, team):
        slot = lax.rem(seat + j, team)
        share(slot, slot).wait_recv()
        earlier = jnp.where(slot < seat, 1, 0)
        sum_of = sum_of + group_in[slot] * jnp.where(upper, 1, earlier)
    row_at = lax.broadcasted_iota(jnp.int32, tally.shape, 0)
    lane_at = lax.broadcasted_iota(jnp.int32, tally.shape, 1)
    chosen = jnp.logical_and(lane_at == 0, lax.rem(row_at, tally.shape[0] // 2) == 0)
    excess = jnp.sum(jnp.where(chosen, sum_of, 0)) - SLOTS * me

    for k in range(SHIFT_MOST, SLOTS):
        out_ref[k] = own[jnp.clip(k - excess, 0, SLOTS - 1)]

    for k in range(SHIFT_MOST):
        out_ref[k] = own[jnp.clip(k - excess, 0, SLOTS - 1)]

    @pl.when(jnp.logical_not(is_first))
    def _():
        rims.wait_recv()
        for k in range(SHIFT_MOST):
            tile(k).wait_recv()
        ends = rim_in[...].astype(jnp.float32)
        for k in range(SHIFT_MOST):
            source = jnp.minimum(
                k + SHIFT_MOST - jnp.clip(excess, 0, SHIFT_MOST), SHIFT_MOST - 1)
            late = jnp.full((PACK, quad), excess, jnp.int32) > k
            second = jnp.full((PACK, quad), source, jnp.int32) == 1
            for g in range(groups):
                span = pl.ds(g * quad, quad)
                for s, line, at in ((0, 0, 0), (1, PACK - 1, side - PACK)):
                    theirs = arrived[source, at:at + PACK, span].astype(jnp.float32)
                    end = jnp.where(
                        second,
                        jnp.broadcast_to(ends[2 + s:3 + s, g * quad:(g + 1) * quad], (PACK, quad)),
                        jnp.broadcast_to(ends[s:s + 1, g * quad:(g + 1) * quad], (PACK, quad)))
                    theirs = jnp.where(line_at == line, end, theirs)
                    mine = out_ref[k, at:at + PACK, span].astype(jnp.float32)
                    out_ref[k, at:at + PACK, span] = (
                        jnp.where(late, theirs, mine).astype(jnp.bfloat16))
        up.wait_send()

    @pl.when(jnp.logical_not(is_last))
    def _():
        down.wait_send()
        rims.wait_send()
        for k in range(SHIFT_MOST):
            tile(k).wait_send()

    @pl.when(has_ahead)
    def _():
        relay.wait_send()

    for j in range(1, team):
        share(lax.rem(seat + j, team), seat).wait_send()


def on_device(slide_pixels, tissue_mask, conv_weight, conv_bias):
    n = lax.axis_size("row")
    band_rows, cols = tissue_mask.shape
    channels = conv_weight.shape[2]
    height = slide_pixels.shape[0]
    side = height // band_rows
    width = side * channels
    quad = 2 * LANES
    team = math.gcd(n, GROUP)
    bf16 = jnp.bfloat16
    dma = pltpu.SemaphoreType.DMA
    anywhere = pl.BlockSpec(memory_space=pl.ANY)
    line = pltpu.VMEM((cols, width), bf16)
    note = pltpu.VMEM((8, LANES), jnp.int32)
    return pl.pallas_call(
        functools.partial(kernel, n, side, channels),
        out_shape=pltpu.VMEM((SLOTS, side, width), bf16),
        in_specs=[anywhere] * 4,
        out_specs=pl.BlockSpec(memory_space=pltpu.VMEM),
        scratch_shapes=[
            pltpu.VMEM((band_rows + 2, cols + 2, side, width), bf16),
            pltpu.VMEM((SLOTS, side, width), bf16),
            pltpu.VMEM((3, side, 2 * (width + quad)), bf16),
            pltpu.VMEM((3, 2 * quad, quad), bf16),
            pltpu.VMEM(conv_weight.shape, bf16),
            pltpu.VMEM((1, channels), bf16),
            pltpu.SMEM((band_rows, cols), jnp.int32),
            line, line, line, line, line, line,
            pltpu.VMEM((SHIFT_MOST, side, width), bf16),
            pltpu.VMEM((SHIFT_MOST, side, width), bf16),
            pltpu.VMEM((2, cols, 1, width), jnp.float32),
            pltpu.VMEM((2 * SHIFT_MOST, width), bf16),
            pltpu.VMEM((2 * SHIFT_MOST, width), bf16),
            note, note, note,
            pltpu.VMEM((team, 8, LANES), jnp.int32),
            dma((band_rows * cols,)), dma((3,)), dma((2,)), dma((2,)),
            dma((SHIFT_MOST,)), dma((SHIFT_MOST,)), dma, dma, dma, dma,
            dma((team,)), dma((team,)),
        ],
        compiler_params=pltpu.CompilerParams(collective_id=0, has_side_effects=True),
    )(slide_pixels, tissue_mask, conv_weight, conv_bias.reshape(1, channels))


def solution(mesh):
    return jax.shard_map(
        on_device,
        mesh=mesh,
        in_specs=(P(("slides", "row"), None), P(("slides", "row"), None), P(), P()),
        out_specs=P(("slides", "row"), None, None),
        check_vma=False,
    )
```

time: 16.9 us -> 13.9 us (0.82)
  the two profiles are of different devices: /device:TPU:8 before, /device:TPU:25 now
where the time goes in v1:
time: 13.9 us; the launch traced here: 13.7 us
  Pallas kernels  12.7 us (91%)
  local copies, waits for them, and re-layouts  0.97 us (7%)
    pallas_call x1, Pallas kernels, on_device(): pl.pallas_call(functools.partial(kernel, n, side, channels), out_shape=pl...  12.7 us
    unnamed x1, local copies, waits for them, and re-layouts  0.97 us

profile of v1, /device:TPU:25, one launch (start us, length us, event | category | flops | bytes accessed | tf_op | source)
XLA Modules:
  0.0 13.7 jit_solution(11302259099102115469)
XLA Ops:
  0.0 12.7 %shard_map.46 = bf16[8,32,2048]{2,1,0:T(8,128)(2,1)S(1)} custom-call(bf16[64,16384]{1,0:T(8,128)(2,1)} %x_any.1, s32[2,8]{1,0:T(2,128)} %mask_any.1, bf16[3,3,64,64]{3,2,1,0:T(8,128)(2,1)} %w_any.1, bf16[1,64]{1,0:T(2,128)(2,1)} %bitcast.1), custom_call_target="tpu_custom_call" | custom-call | tf_op jit(solution)/shard_map/pallas_call | solution.py:409
  12.8 1.0 %copy.6 = bf16[8,32,2048]{2,1,0:T(8,128)(2,1)} copy(bf16[8,32,2048]{2,1,0:T(8,128)(2,1)S(1)} %shard_map.46) | data formatting | bytes 2097152

commit v2 on v1

v2 whole, which is shorter than its diff:
```python
import functools

import jax
import jax.numpy as jnp
from jax import lax
from jax.experimental import pallas as pl
from jax.experimental.pallas import tpu as pltpu
from jax.sharding import PartitionSpec as P

SLOTS = 8
SHIFT_MOST = 2
LANES = 128
PACK = 16
TEAM = 4
MESH = pl.DeviceIdType.MESH


def kernel(
    n, side, channels,
    x_any, mask_any, w_any, b_any, out_ref,
    image, own, rows3, wide, w_ref, b_ref, mask_s,
    lines, row_first, row_last, halo_top, halo_bot,
    onward, arrived, edge, below,
    top_out, top_in, end_out, end_in, pick_out, pick_in,
    tally, mate, pair, pair_in, chain_out, chain_in,
    x_sem, in_sem, halo_send, halo_recv, tile_send, tile_recv, rim_send, rim_recv,
    mate_send, mate_recv, pair_send, pair_recv, chain_send, chain_recv,
):
    band_rows, cols = mask_s.shape
    width = side * channels
    tiles = band_rows * cols
    quad = 2 * LANES
    groups = width // quad
    per = quad // channels
    half = LANES // channels
    me = lax.axis_index("row")
    seat = lax.rem(me, TEAM)
    base = me - seat
    deep = lax.div(base, TEAM)
    odd = lax.rem(me, 2) == 1
    even = jnp.logical_not(odd)
    chip = lax.div(seat, 2)
    is_first = me == 0
    is_last = me == n - 1
    has_back = me >= TEAM
    has_ahead = base + TEAM < n

    barrier = pltpu.get_barrier_semaphore()

    def greet(target):
        pl.semaphore_signal(barrier, inc=1, device_id={"row": target}, device_id_type=MESH)

    @pl.when(odd)
    def _():
        greet(me - 1)

    @pl.when(jnp.logical_not(is_last))
    def _():
        greet(me + 1)

    @pl.when(seat == 2)
    def _():
        greet(me - 1)

    @pl.when(seat == 3)
    def _():
        greet(me - 2)

    @pl.when(has_back)
    def _():
        greet(base - 1)
        greet(base - 3)

    def fetch(r, c):
        return pltpu.make_async_copy(
            x_any.at[pl.ds(r * side, side), pl.ds(c * width, width)],
            image.at[r + 1, c + 1],
            x_sem.at[r * cols + c],
        )

    get_mask = pltpu.make_async_copy(mask_any, mask_s, in_sem.at[0])
    get_w = pltpu.make_async_copy(w_any, w_ref, in_sem.at[1])
    get_b = pltpu.make_async_copy(b_any, b_ref, in_sem.at[2])
    get_mask.start()
    get_w.start()
    get_b.start()
    for c in range(cols):
        for r in range(band_rows):
            fetch(r, c).start()

    for r in range(1, band_rows + 1):
        image[r, 0, :, width - LANES:width] = jnp.zeros((side, LANES), jnp.bfloat16)
        image[r, cols + 1, :, 0:LANES] = jnp.zeros((side, LANES), jnp.bfloat16)
    for c in range(cols + 2):
        image[0, c, side - PACK:side, :] = jnp.zeros((PACK, width), jnp.bfloat16)
        image[band_rows + 1, c, 0:PACK, :] = jnp.zeros((PACK, width), jnp.bfloat16)

    @pl.when(is_first)
    def _():
        halo_top[...] = jnp.zeros_like(halo_top)

    @pl.when(is_last)
    def _():
        halo_bot[...] = jnp.zeros_like(halo_bot)

    @pl.when(even)
    def _():
        mate[...] = jnp.zeros_like(mate)

    @pl.when(seat < 2)
    def _():
        pair_in[...] = jnp.zeros_like(pair_in)

    @pl.when(jnp.logical_not(has_back))
    def _():
        chain_in[...] = jnp.zeros_like(chain_in)

    get_mask.wait()
    seen = []
    for r in range(band_rows):
        for c in range(cols):
            seen.append(mask_s[r, c] + (seen[-1] if seen else 0))
    count = seen[-1]

    def place(rank):
        spot = jnp.int32(0)
        row = jnp.int32(0)
        for t in range(tiles - 1):
            past = jnp.where(seen[t] <= rank, 1, 0)
            spot = spot + past
            if t % cols == cols - 1:
                row = row + past
        return row, spot - row * cols

    ahead = {"row": lax.rem(me + 1, n)}
    behind = {"row": lax.rem(me + n - 1, n)}

    def remote(source, target, send, recv, device):
        return pltpu.make_async_remote_copy(
            source, target, send, recv, device_id=device, device_id_type=MESH)

    tell_mate = remote(tally, mate, mate_send, mate_recv, ahead)
    down = remote(row_last, halo_top, halo_send.at[0], halo_recv.at[0], ahead)
    up = remote(row_first, halo_bot, halo_send.at[1], halo_recv.at[1], behind)
    tile = [
        remote(onward.at[k], arrived.at[k], tile_send.at[k], tile_recv.at[k], ahead)
        for k in range(SHIFT_MOST)
    ]
    rims = [
        remote(source, target, rim_send.at[i], rim_recv.at[i], ahead)
        for i, (source, target) in enumerate(
            ((top_out, top_in), (end_out, end_in), (pick_out, pick_in)))
    ]

    def tell_pair(j):
        return remote(pair, pair_in, pair_send.at[j], pair_recv, {"row": base + 2 + j})

    def relay(j, slot):
        return remote(
            chain_out, chain_in.at[slot], chain_send.at[j], chain_recv.at[slot],
            {"row": lax.rem(base + TEAM + j, n)})

    tally[...] = jnp.full(tally.shape, count, jnp.int32)

    @pl.when(even)
    def _():
        pl.semaphore_wait(barrier, 1 + jnp.where(is_first, 0, 1))
        tell_mate.start()

    get_w.wait()
    none = jnp.zeros((channels, channels), jnp.bfloat16)
    for dy in range(3):
        taps = [w_ref[dy, 0], w_ref[dy, 1], w_ref[dy, 2]]
        for p in range(2 * per):
            for q in range(per // half):
                u = p - half - half * q
                parts = [taps[u + 1 - o] if 0 <= u + 1 - o <= 2 else none for o in range(half)]
                wide[dy, p * channels:(p + 1) * channels, q * LANES:(q + 1) * LANES] = (
                    jnp.concatenate(parts, axis=1)
                )
    get_b.wait()
    bias = b_ref[...].astype(jnp.float32)
    bias = jnp.concatenate([bias] * per, axis=1)

    for c in range(cols):
        for r in range(band_rows):
            fetch(r, c).wait()
            keep = jnp.full((side, LANES), mask_s[r, c], jnp.int32).astype(jnp.float32)
            keep = keep.astype(jnp.bfloat16)
            for k in range(width // LANES):
                at = (r + 1, c + 1, slice(None), pl.ds(k * LANES, LANES))
                image[at] = image[at] * keep
        first = image[1, c + 1, 0:PACK].astype(jnp.float32)
        last = image[band_rows, c + 1, side - PACK:side].astype(jnp.float32)
        lines[0, c:c + 1, :] = first[0:1]
        lines[1, c:c + 1, :] = first[1:2]
        lines[2, c:c + 1, :] = last[PACK - 2:PACK - 1]
        lines[3, c:c + 1, :] = last[PACK - 1:PACK]
    row_first[...] = lines[0].astype(jnp.bfloat16)
    row_last[...] = lines[3].astype(jnp.bfloat16)

    @pl.when(odd)
    def _():
        pl.semaphore_wait(
            barrier, 1 + jnp.where(seat == 1, 2, 0) + jnp.where(has_ahead, TEAM, 0))

    @pl.when(jnp.logical_not(is_last))
    def _():
        down.start()

    def pass_on(before):
        chain_out[...] = before + pair[...]
        for j in range(TEAM):
            relay(j, chip).start()

    @pl.when(odd)
    def _():
        tell_mate.wait_recv()
        pair[...] = tally[...] + mate[...]

        @pl.when(seat == 1)
        def _():
            for j in range(2):
                tell_pair(j).start()

        @pl.when(jnp.logical_and(has_ahead, jnp.logical_not(has_back)))
        def _():
            pass_on(jnp.zeros(pair.shape, jnp.int32))

    @pl.when(jnp.logical_not(is_first))
    def _():
        up.start()

    def convolve(spots, put):
        for i, (r, c) in enumerate(spots):
            for k in range(width // LANES + 2):
                if k == 0:
                    at, lane = c, width - LANES
                elif k <= width // LANES:
                    at, lane = c + 1, (k - 1) * LANES
                else:
                    at, lane = c + 2, 0
                lane = slice(lane, lane + LANES)
                block = image[r + 1, at, :, lane]
                above = image[r, at, side - PACK:side, lane].astype(jnp.float32)
                beneath = image[r + 2, at, 0:PACK, lane].astype(jnp.float32)
                block32 = block.astype(jnp.float32)
                span = pl.ds(i * (groups + 1) * quad + k * LANES, LANES)
                rows3[0, :, span] = jnp.concatenate(
                    [above[PACK - 1:PACK], block32[0:side - 1]], axis=0).astype(jnp.bfloat16)
                rows3[1, :, span] = block
                rows3[2, :, span] = jnp.concatenate(
                    [block32[1:side], beneath[0:1]], axis=0).astype(jnp.bfloat16)
        starts = [(i * (groups + 1) + g) * quad for i in range(len(spots)) for g in range(groups)]
        left_side = jnp.concatenate([jnp.concatenate(
            [rows3[dy, :, s:s + 2 * quad] for s in starts], axis=0)
            for dy in range(3)], axis=1)
        total = jnp.dot(left_side, wide[...].reshape(6 * quad, quad),
            preferred_element_type=jnp.float32) + bias
        for i in range(len(spots)):
            for g in range(groups):
                at = (i * groups + g) * side
                put(i, g, total[at:at + side])

    leaving = [place(count - SHIFT_MOST + k) for k in range(SHIFT_MOST)]
    for k in range(SHIFT_MOST):
        def put_onward(i, g, value, k=k):
            span = slice(g * quad, (g + 1) * quad)
            onward[k, :, span] = value.astype(jnp.bfloat16)
            end_out[k:k + 1, span] = value[side - 1:side]

        convolve([leaving[k]], put_onward)

        @pl.when(jnp.logical_not(is_last))
        def _(k=k):
            tile[k].start()

    def stack(line):
        blank = jnp.zeros((1, LANES), jnp.float32)
        before = jnp.concatenate([blank, line[0:cols - 1, width - LANES:width]], axis=0)
        after = jnp.concatenate([line[1:cols, 0:LANES], blank], axis=0)
        line = jnp.concatenate([before, line, after], axis=1)
        return jnp.concatenate(
            [line[:, g * quad:(g + 2) * quad] for g in range(groups)], axis=0).astype(jnp.bfloat16)

    def rim(s, trio):
        found = jnp.dot(
            jnp.concatenate([stack(line) for line in trio], axis=1),
            wide[...].reshape(6 * quad, quad), preferred_element_type=jnp.float32) + bias
        for g in range(groups):
            for c in range(cols):
                edge[s, c, :, g * quad:(g + 1) * quad] = found[g * cols + c:g * cols + c + 1]

    def send_rims():
        @pl.when(jnp.logical_not(is_first))
        def _():
            down.wait_recv()

        rim(0, (halo_top[...].astype(jnp.float32), lines[0], lines[1]))
        row_at = lax.broadcasted_iota(jnp.int32, (cols, LANES), 0)
        tops, picks = [], []
        for k, (r, c) in enumerate(leaving):
            at_top = jnp.full((1, width), r, jnp.int32) == 0
            tops.append(jnp.where(
                at_top, edge[0, c], onward[k, 0:PACK].astype(jnp.float32)[0:1]))
            at_end = jnp.full((cols, LANES), r, jnp.int32) == band_rows - 1
            picks.append(jnp.where(jnp.logical_and(at_end, row_at == c), 1.0, 0.0))
        top_out[...] = jnp.concatenate(tops, axis=0).astype(jnp.bfloat16)
        pick_out[...] = jnp.concatenate(picks, axis=0).astype(jnp.bfloat16)

        @pl.when(jnp.logical_not(is_last))
        def _():
            for copy in rims:
                copy.start()

    duo = 2
    duos = SLOTS // duo
    turn = (deep - 1) * 2
    relays = jnp.logical_and(odd, jnp.logical_and(has_back, has_ahead))

    def take_and_pass():
        relay(0, chip).wait_recv()
        pass_on(chain_in[chip])

    def several(j, carry):
        @pl.when(jnp.logical_and(relays, turn == j))
        def _():
            take_and_pass()

        @pl.when(jnp.logical_and(odd, j == 1))
        def _():
            send_rims()

        def put_own(i, g, value):
            own[j * duo + i, :, g * quad:(g + 1) * quad] = value.astype(jnp.bfloat16)

        convolve([place(j * duo + i) for i in range(duo)], put_own)
        return carry

    lax.fori_loop(0, duos, several, 0)

    @pl.when(jnp.logical_and(relays, turn >= duos))
    def _():
        take_and_pass()

    @pl.when(even)
    def _():
        send_rims()

    adds = jnp.dot(stack(lines[0]), wide[2], preferred_element_type=jnp.float32)
    for g in range(groups):
        below[:, g * quad:(g + 1) * quad] = adds[g * cols:(g + 1) * cols]

    @pl.when(jnp.logical_not(is_last))
    def _():
        up.wait_recv()

    rim(1, (lines[2], lines[3], halo_bot[...].astype(jnp.float32)))

    line_at = lax.broadcasted_iota(jnp.int32, (PACK, quad), 0)

    def finish(j, carry):
        r, c = place(j)
        rows = jnp.full((PACK, quad), r, jnp.int32)
        at_top = jnp.logical_and(rows == 0, line_at == 0)
        at_end = jnp.logical_and(rows == band_rows - 1, line_at == PACK - 1)
        for g in range(groups):
            span = pl.ds(g * quad, quad)
            for s, where, at in ((0, at_top, 0), (1, at_end, side - PACK)):
                old = own[j, at:at + PACK, span].astype(jnp.float32)
                new = jnp.broadcast_to(edge[s, c, :, span], (PACK, quad))
                own[j, at:at + PACK, span] = jnp.where(where, new, old).astype(jnp.bfloat16)
        return carry

    lax.fori_loop(0, SLOTS, finish, 0)

    @pl.when(seat >= 2)
    def _():
        tell_pair(0).wait_recv()

    @pl.when(has_back)
    def _():
        for slot in range(2):
            @pl.when(jnp.logical_or(jnp.logical_not(relays), chip != slot))
            def _(slot=slot):
                relay(0, slot).wait_recv()

    excess = chain_in[0] + chain_in[1] + pair_in[...] + mate[...] - SLOTS * me
    excess32 = jnp.concatenate([excess] * (PACK // excess.shape[0]), axis=0).astype(jnp.float32)
    excess16 = excess32.astype(jnp.bfloat16)
    by_one = excess16 == jnp.bfloat16(1)
    by_two = excess16 == jnp.bfloat16(2)

    for k in range(SHIFT_MOST, SLOTS):
        for at in range(0, side, PACK):
            for lane in range(0, width, LANES):
                spot = (slice(at, at + PACK), slice(lane, lane + LANES))
                out_ref[(k,) + spot] = jnp.where(
                    by_two, own[(k - 2,) + spot],
                    jnp.where(by_one, own[(k - 1,) + spot], own[(k,) + spot]))

    @pl.when(is_first)
    def _():
        for k in range(SHIFT_MOST):
            out_ref[k] = own[k]

    @pl.when(jnp.logical_not(is_first))
    def _():
        for copy in tile + rims:
            copy.wait_recv()
        row16 = lax.broadcasted_iota(jnp.int32, (PACK, LANES), 0)
        one = excess32 == 1
        two = excess32 == 2
        for lane in range(0, width, LANES):
            span = slice(lane, lane + LANES)
            tops = top_in[:, span].astype(jnp.float32)
            for at, line in ((0, 0), (side - PACK, PACK - 1)):
                theirs = []
                for k in range(SHIFT_MOST):
                    if at == 0:
                        rim_row = tops[k:k + 1]
                    else:
                        pick = pick_in[...].astype(jnp.float32)[k * cols:(k + 1) * cols]
                        rim_row = end_in[k:k + 1, span] + jnp.sum(
                            pick * below[:, span], axis=0, keepdims=True)
                    theirs.append(jnp.where(
                        row16 == line, jnp.broadcast_to(rim_row, (PACK, LANES)),
                        arrived[k, at:at + PACK, span].astype(jnp.float32)))
                mine = [own[k, at:at + PACK, span].astype(jnp.float32) for k in range(SHIFT_MOST)]
                out_ref[0, at:at + PACK, span] = jnp.where(
                    two, theirs[0], jnp.where(one, theirs[1], mine[0])).astype(jnp.bfloat16)
                out_ref[1, at:at + PACK, span] = jnp.where(
                    two, theirs[1], jnp.where(one, mine[0], mine[1])).astype(jnp.bfloat16)
        up.wait_send()

    @pl.when(jnp.logical_not(is_last))
    def _():
        down.wait_send()
        for copy in tile + rims:
            copy.wait_send()

    @pl.when(even)
    def _():
        tell_mate.wait_send()

    @pl.when(seat == 1)
    def _():
        for j in range(2):
            tell_pair(j).wait_send()

    @pl.when(jnp.logical_and(odd, has_ahead))
    def _():
        for j in range(TEAM):
            relay(j, chip).wait_send()


def on_device(slide_pixels, tissue_mask, conv_weight, conv_bias):
    n = lax.axis_size("row")
    band_rows, cols = tissue_mask.shape
    channels = conv_weight.shape[2]
    height = slide_pixels.shape[0]
    side = height // band_rows
    width = side * channels
    quad = 2 * LANES
    bf16 = jnp.bfloat16
    f32 = jnp.float32
    dma = pltpu.SemaphoreType.DMA
    anywhere = pl.BlockSpec(memory_space=pl.ANY)
    line = pltpu.VMEM((cols, width), bf16)
    note = pltpu.VMEM((8, LANES), jnp.int32)
    return pl.pallas_call(
        functools.partial(kernel, n, side, channels),
        out_shape=pltpu.VMEM((SLOTS, side, width), bf16),
        in_specs=[anywhere] * 4,
        out_specs=pl.BlockSpec(memory_space=pltpu.VMEM),
        scratch_shapes=[
            pltpu.VMEM((band_rows + 2, cols + 2, side, width), bf16),
            pltpu.VMEM((SLOTS, side, width), bf16),
            pltpu.VMEM((3, side, 2 * (width + quad)), bf16),
            pltpu.VMEM((3, 2 * quad, quad), bf16),
            pltpu.VMEM(conv_weight.shape, bf16),
            pltpu.VMEM((1, channels), bf16),
            pltpu.SMEM((band_rows, cols), jnp.int32),
            pltpu.VMEM((4, cols, width), f32),
            line, line, line, line,
            pltpu.VMEM((SHIFT_MOST, side, width), bf16),
            pltpu.VMEM((SHIFT_MOST, side, width), bf16),
            pltpu.VMEM((2, cols, 1, width), f32),
            pltpu.VMEM((cols, width), f32),
            pltpu.VMEM((SHIFT_MOST, width), bf16),
            pltpu.VMEM((SHIFT_MOST, width), bf16),
            pltpu.VMEM((SHIFT_MOST, width), f32),
            pltpu.VMEM((SHIFT_MOST, width), f32),
            pltpu.VMEM((SHIFT_MOST * cols, LANES), bf16),
            pltpu.VMEM((SHIFT_MOST * cols, LANES), bf16),
            note, note, note, note, note,
            pltpu.VMEM((2, 8, LANES), jnp.int32),
            dma((band_rows * cols,)), dma((3,)), dma((2,)), dma((2,)),
            dma((SHIFT_MOST,)), dma((SHIFT_MOST,)), dma((3,)), dma((3,)),
            dma, dma, dma((2,)), dma, dma((TEAM,)), dma((2,)),
        ],
        compiler_params=pltpu.CompilerParams(collective_id=0, has_side_effects=True),
    )(slide_pixels, tissue_mask, conv_weight, conv_bias.reshape(1, channels))


def solution(mesh):
    return jax.shard_map(
        on_device,
        mesh=mesh,
        in_specs=(P(("slides", "row"), None), P(("slides", "row"), None), P(), P()),
        out_specs=P(("slides", "row"), None, None),
        check_vma=False,
    )
```

time: 13.9 us -> 11.7 us (0.84)
  Pallas kernels: 12.7 us -> 10.6 us
    pallas_call x1, Pallas kernels: 12.7 us -> 10.6 us  [on_device(): pl.pallas_call(functools.partial(kernel, n, side, channels), out_shape=pl...]
where the time goes in v2:
time: 11.7 us; the launch traced here: 11.6 us
  Pallas kernels  10.6 us (91%)
  local copies, waits for them, and re-layouts  0.97 us (8%)
    pallas_call x1, Pallas kernels, on_device(): pl.pallas_call(functools.partial(kernel, n, side, channels), out_shape=pl...  10.6 us
    unnamed x1, local copies, waits for them, and re-layouts  0.97 us

profile of v2, /device:TPU:25, one launch (start us, length us, event | category | flops | bytes accessed | tf_op | source)
XLA Modules:
  0.0 11.6 jit_solution(9127035870008175453)
XLA Ops:
  0.0 10.6 %shard_map.46 = bf16[8,32,2048]{2,1,0:T(8,128)(2,1)S(1)} custom-call(bf16[64,16384]{1,0:T(8,128)(2,1)} %x_any.1, s32[2,8]{1,0:T(2,128)} %mask_any.1, bf16[3,3,64,64]{3,2,1,0:T(8,128)(2,1)} %w_any.1, bf16[1,64]{1,0:T(2,128)(2,1)} %bitcast.1), custom_call_target="tpu_custom_call" | custom-call | tf_op jit(solution)/shard_map/pallas_call | solution.py:471
  10.6 1.0 %copy.6 = bf16[8,32,2048]{2,1,0:T(8,128)(2,1)} copy(bf16[8,32,2048]{2,1,0:T(8,128)(2,1)S(1)} %shard_map.46) | data formatting | bytes 2097152
